TPU v7x, 32 devices: a whole 2x2x4 slice. The times are simulated.
32 devices in a mesh: row: 8 (over y, x, core), col: 4 (over z).
Axes of the slice: x: 2, y: 2, z: 4, core: 2. Of those that a mesh axis runs over, the one named last changes fastest.
Arguments:
- right_side: float32 [5, 8, 4, 32, 128], P(None, 'row', 'col'), may hold values from -6 to 6
- diag_blocks: float32 [5, 8, 4, 128, 128], P(None, 'row', 'col'), may hold values from -1 to 2, as said below
- off_blocks: float32 [8, 4, 4, 8, 128, 128], P('row', 'col'), may hold values from -0.1875 to 0.1875
- slot_target: int32 [8, 4, 4, 8], P('row', 'col'), may hold values from 0 to 7
- slot_level: int32 [8, 4, 4, 8], P('row', 'col'), may hold values from 0 to 3, as said below
- slot_position: int32 [8, 4, 4, 8], P('row', 'col'), may hold values from 0 to 3
- slot_count: int32 [8, 4, 4], P('row', 'col'), may hold values from 1 to 8
Outputs:
- solution: float32 [5, 8, 4, 32, 128], P(None, 'row', 'col')
Inputs may be any that keep to these rules, and one draw needn't show every extreme that they name: slot_level[..., m, s] is a level below the target level m + 1. slot_target names a row group. slot_position names a column group. `diag_blocks`: each diagonal block is lower triangular with its diagonal between 1 and 2 and strictly lower entries of size at most 1 / sqrt(128).
All inputs are finite; a program needn't handle non-finite values.
Results may differ from a plain program's by a relative error of at most 0.0001.
Values sent between devices are 32-bit elements; how exact they have to be, the bound alone decides.
A program may use at most 64 MiB of HBM per device.

v0:
```python
import jax
import jax.numpy as jnp
from jax import lax
from jax.sharding import PartitionSpec as P


def solve_block(diagonal, right_rows):
    return jax.scipy.linalg.solve_triangular(diagonal, right_rows.T, lower=True).T


def slot_products(gathered, blocks, source_ids, source_cols, weights):
    operands = gathered[source_ids, source_cols] * weights[:, None, None]
    return jnp.einsum("snb,sab->sna", operands, blocks, precision=lax.Precision.HIGHEST)


def per_device(
    right_side, diag_blocks, off_blocks, slot_target, slot_level, slot_position, slot_count
):
    right_rows = right_side[:, 0, 0]
    diagonal = diag_blocks[:, 0, 0]
    blocks = off_blocks[0, 0]
    targets = slot_target[0, 0]
    source_levels = slot_level[0, 0]
    positions = slot_position[0, 0]
    counts = slot_count[0, 0]
    level_total = right_rows.shape[0]
    slot_total = blocks.shape[1]
    col_count = lax.axis_size("col")
    group_count = lax.axis_size("row")
    gathered = jnp.zeros((level_total, col_count) + right_rows.shape[1:], jnp.float32)
    slot_ids = jnp.arange(slot_total, dtype=jnp.int32)
    group_ids = jnp.arange(group_count, dtype=jnp.int32)
    solved = []
    pending = None
    for level_now in range(level_total):
        if level_now == 0:
            reduced = jnp.zeros(right_rows.shape[1:], jnp.float32)
        else:
            target_now = targets[level_now - 1]
            selector = (target_now[:, None] == group_ids[None, :]).astype(jnp.float32)
            by_target = jnp.einsum(
                "st,sna->tna", selector, pending, precision=lax.Precision.HIGHEST
            )
            received = lax.all_to_all(by_target, "row", split_axis=0, concat_axis=0, tiled=True)
            reduced = jnp.sum(received, axis=0)
        current = solve_block(diagonal[level_now], right_rows[level_now] - reduced)
        solved.append(current)
        if level_now + 1 < level_total:
            source_ids = source_levels[level_now]
            source_cols = positions[level_now]
            active = slot_ids < counts[level_now]
            shared = lax.all_gather(current[None], "col", axis=0, tiled=True)
            gathered = gathered.at[level_now].set(shared)
            pending = slot_products(
                gathered, blocks[level_now], source_ids, source_cols, active.astype(jnp.float32)
            )
    return jnp.stack(solved)[:, None, None]


def solution(mesh):
    placed = (
        P(None, "row", "col", None, None),
        P(None, "row", "col", None, None),
        P("row", "col", None, None, None, None),
        P("row", "col", None, None),
        P("row", "col", None, None),
        P("row", "col", None, None),
        P("row", "col", None),
    )
    return jax.shard_map(
        per_device,
        mesh=mesh,
        in_specs=placed,
        out_specs=P(None, "row", "col", None, None),
        check_vma=False,
    )
```

profile of v0, /device:TPU:0, one launch (start us, length us, event | category | flops | bytes accessed | tf_op | source)
XLA Modules:
  0.0 140.1 jit_solution(848645339061681222)
XLA Ops:
  0.0 0.9 slice_bitcast_fusion
  0.9 1.5 %fusion.89 = (s32[1,1,1]{2,1,0:T(1,128)}, s32[1,1,1]{2,1,0:T(1,128)}, s32[1,1,1]{2,1,0:T(1,128)}, s32[1,1,1]{2,1,0:T(1,128)}) fusion(s32[1,1,4]{2,1,0:T(1,128)} %param.23), kind=kLoop, calls=%fused_computation.127 | loop fusion | bytes 32 | tf_op jit(solution)/shard_map/slice | solution.py:51
  2.9 1.0 fusion.26
  3.9 9.8 %custom-call.15 = f32[1,128,128]{1,2,0:T(8,128)S(1)} custom-call(f32[1,128,128]{2,1,0:T(8,128)S(1)} %get-tuple-element.57), custom_call_target="InvertDiagBlocksLowerTriangular" | custom-call | tf_op jit(solution)/shard_map/jit(_solve_triangular)/triangular_solve | solution.py:8
  13.7 0.9 bitcast_dynamic-update-slice_fusion.3
  14.6 14.9 %all-gather = f32[128,128]{1,0:T(8,128)S(1)} all-gather(f32[32,128]{1,0:T(8,128)S(1)} %bitcast.213), channel_id=2, replica_groups=mesh['row'=8,'col'=4] {'col'}, dimensions={0}, use_global_device_ids=true | all-gather | bytes 81920 | tf_op jit(solution)/shard_map/all_gather | solution.py:52
  29.5 0.8 fusion.85
  31.0 2.0 %fusion.7 = f32[8,32,128]{2,1,0:T(8,128)S(1)} fusion(f32[1,1,4,8,128,128]{5,4,3,2,1,0:T(8,128)} %param.19, f32[8,32,128]{2,1,0:T(8,128)S(1)} %gather_fusion, f32[8]{0:T(128)S(1)} %compare_convert_fusion.3), kind=kOutput, calls=%fused_computation.12 | convolution fusion | flops 50364416 | bytes 786464 | tf_op jit(solution)/shard_map/snb,sab->sna/dot_general | solution.py:13
  33.4 0.7 copy.11
  34.0 3.7 %all-to-all-start = ((f32[8,32,128]{2,1,0:T(8,128)}), f32[8,32,128]{2,1,0:T(8,128)S(1)}, u32[]{:S(2)}, u32[]{:S(2)}) async-start(f32[8,32,128]{2,1,0:T(8,128)} %copy.11), calls=%async_computation | async-start | bytes 262144 | tf_op jit(solution)/shard_map/all_to_all | solution.py:44
  37.8 9.8 %custom-call.16 = f32[1,128,128]{1,2,0:T(8,128)S(1)} custom-call(f32[1,128,128]{2,1,0:T(8,128)S(1)} %get-tuple-element.56), custom_call_target="InvertDiagBlocksLowerTriangular" | custom-call | tf_op jit(solution)/shard_map/jit(_solve_triangular)/triangular_solve | solution.py:8
  48.4 13.1 %all-gather.1 = f32[128,128]{1,0:T(8,128)S(1)} all-gather(f32[32,128]{1,0:T(8,128)S(1)} %bitcast.214), channel_id=3, replica_groups=mesh['row'=8,'col'=4] {'col'}, dimensions={0}, use_global_device_ids=true | all-gather | bytes 81920 | tf_op jit(solution)/shard_map/all_gather | solution.py:52
  62.2 1.0 fusion.5
  64.1 4.2 %all-to-all-start.1 = ((f32[8,32,128]{2,1,0:T(8,128)}), f32[8,32,128]{2,1,0:T(8,128)S(1)}, u32[]{:S(2)}, u32[]{:S(2)}) async-start(f32[8,32,128]{2,1,0:T(8,128)} %copy.13), calls=%async_computation.1 | async-start | bytes 262144 | tf_op jit(solution)/shard_map/all_to_all | solution.py:44
  68.3 9.8 %custom-call.17 = f32[1,128,128]{1,2,0:T(8,128)S(1)} custom-call(f32[1,128,128]{2,1,0:T(8,128)S(1)} %get-tuple-element.55), custom_call_target="InvertDiagBlocksLowerTriangular" | custom-call | tf_op jit(solution)/shard_map/jit(_solve_triangular)/triangular_solve | solution.py:8
  79.0 13.1 %all-gather.2 = f32[128,128]{1,0:T(8,128)S(1)} all-gather(f32[32,128]{1,0:T(8,128)S(1)} %bitcast.215), channel_id=4, replica_groups=mesh['row'=8,'col'=4] {'col'}, dimensions={0}, use_global_device_ids=true | all-gather | bytes 81920 | tf_op jit(solution)/shard_map/all_gather | solution.py:52
  92.7 1.0 fusion.3
  94.0 0.7 copy.15
  94.7 4.2 %all-to-all-start.2 = ((f32[8,32,128]{2,1,0:T(8,128)}), f32[8,32,128]{2,1,0:T(8,128)S(1)}, u32[]{:S(2)}, u32[]{:S(2)}) async-start(f32[8,32,128]{2,1,0:T(8,128)} %copy.15), calls=%async_computation.2 | async-start | bytes 262144 | tf_op jit(solution)/shard_map/all_to_all | solution.py:44
  98.9 9.8 %custom-call.18 = f32[1,128,128]{1,2,0:T(8,128)S(1)} custom-call(f32[1,128,128]{2,1,0:T(8,128)S(1)} %get-tuple-element.58), custom_call_target="InvertDiagBlocksLowerTriangular" | custom-call | tf_op jit(solution)/shard_map/jit(_solve_triangular)/triangular_solve | solution.py:8
  109.5 13.1 %all-gather.3 = f32[128,128]{1,0:T(8,128)S(1)} all-gather(f32[32,128]{1,0:T(8,128)S(1)} %bitcast.216), channel_id=5, replica_groups=mesh['row'=8,'col'=4] {'col'}, dimensions={0}, use_global_device_ids=true | all-gather | bytes 81920 | tf_op jit(solution)/shard_map/all_gather | solution.py:52
  123.3 1.0 fusion.1
  125.2 4.2 %all-to-all-start.3 = ((f32[8,32,128]{2,1,0:T(8,128)}), f32[8,32,128]{2,1,0:T(8,128)S(1)}, u32[]{:S(2)}, u32[]{:S(2)}) async-start(f32[8,32,128]{2,1,0:T(8,128)} %copy.17), calls=%async_computation.3 | async-start | bytes 262144 | tf_op jit(solution)/shard_map/all_to_all | solution.py:44
  129.4 9.8 %custom-call.19 = f32[1,128,128]{1,2,0:T(8,128)S(1)} custom-call(f32[1,128,128]{2,1,0:T(8,128)S(1)} %get-tuple-element.54), custom_call_target="InvertDiagBlocksLowerTriangular" | custom-call | tf_op jit(solution)/shard_map/jit(_solve_triangular)/triangular_solve | solution.py:8
  (36 shorter events, 8.9 us)
Async XLA Ops:
  0.0 48.2 %copy-start.1 = (f32[5,1,1,32,128]{4,3,2,1,0:T(8,128)S(1)}, f32[5,1,1,32,128]{4,3,2,1,0:T(8,128)}, u32[]{:S(2)}) copy-start(f32[5,1,1,32,128]{4,3,2,1,0:T(8,128)} %param.17) | copy-start | bytes 245764
  0.0 62.1 %copy-start = (f32[1,1,4,8,128,128]{5,4,3,2,1,0:T(8,128)S(1)}, f32[1,1,4,8,128,128]{5,4,3,2,1,0:T(8,128)}, u32[]{:S(2)}) copy-start(f32[1,1,4,8,128,128]{5,4,3,2,1,0:T(8,128)} %param.19) | copy-start | bytes 6291460
  34.0 14.2 %all-to-all-start = ((f32[8,32,128]{2,1,0:T(8,128)}), f32[8,32,128]{2,1,0:T(8,128)S(1)}, u32[]{:S(2)}, u32[]{:S(2)}) async-start(f32[8,32,128]{2,1,0:T(8,128)} %copy.11), calls=%async_computation | async-start | bytes 262144 | tf_op jit(solution)/shard_map/all_to_all | solution.py:44
  64.1 14.6 %all-to-all-start.1 = ((f32[8,32,128]{2,1,0:T(8,128)}), f32[8,32,128]{2,1,0:T(8,128)S(1)}, u32[]{:S(2)}, u32[]{:S(2)}) async-start(f32[8,32,128]{2,1,0:T(8,128)} %copy.13), calls=%async_computation.1 | async-start | bytes 262144 | tf_op jit(solution)/shard_map/all_to_all | solution.py:44
  94.7 14.7 %all-to-all-start.2 = ((f32[8,32,128]{2,1,0:T(8,128)}), f32[8,32,128]{2,1,0:T(8,128)S(1)}, u32[]{:S(2)}, u32[]{:S(2)}) async-start(f32[8,32,128]{2,1,0:T(8,128)} %copy.15), calls=%async_computation.2 | async-start | bytes 262144 | tf_op jit(solution)/shard_map/all_to_all | solution.py:44
  125.2 14.0 %all-to-all-start.3 = ((f32[8,32,128]{2,1,0:T(8,128)}), f32[8,32,128]{2,1,0:T(8,128)S(1)}, u32[]{:S(2)}, u32[]{:S(2)}) async-start(f32[8,32,128]{2,1,0:T(8,128)} %copy.17), calls=%async_computation.3 | async-start | bytes 262144 | tf_op jit(solution)/shard_map/all_to_all | solution.py:44
  139.4 0.6 copy-start.2
where the time goes:
time: 141 us; the launch traced here: 140 us
  blocking collectives  54.3 us (39%)
  other arithmetic  53.4 us (38%)
  starting transfers between devices  16.3 us (12%)
  local copies, waits for them, and re-layouts  8.02 us (6%)
  matrix products  7.75 us (5%)
    all_gather x4, blocking collectives, per_device(): shared = lax.all_gather(current[None], 'col', axis=0, tiled=True)  54.3 us
    another operation x6, other arithmetic, solve_block(): jax.scipy.linalg.solve_triangular(diagonal, right_rows.T, lower=True)  50 us
    all_to_all x4, starting transfers between devices, per_device(): lax.all_to_all(by_target, 'row', split_axis=0, concat_axis=0, tiled=True)  16.3 us
    dot_general x4, matrix products, slot_products(): jnp.einsum('snb,sab->sna', operands, blocks, precision=lax.Precision.HIGH...  4.89 us
  transfers between devices with their start and end apart: 4, of which 0 were waited for; matrix products, arithmetic and copies ran while one was open for 29% of the time, Pallas kernels for 0%

commit v1 on v0

v1 whole, which is shorter than its diff:
```python
import functools

import jax
import jax.numpy as jnp
from jax import lax
from jax.experimental import pallas as pl
from jax.experimental.pallas import tpu as pltpu
from jax.sharding import PartitionSpec as P

F32 = jnp.float32
BF16 = jnp.bfloat16
SEED_BLOCK = 32
CHAINS = 1


def split_parts(value):
    high = value.astype(BF16)
    return high, (value - high.astype(F32)).astype(BF16)


def exact_dot(left, right):
    return jnp.dot(left, right, precision=lax.Precision.HIGHEST, preferred_element_type=F32)


def unit_upper_inverse(strict):
    size = strict.shape[0]
    row_ids = lax.broadcasted_iota(jnp.int32, (size, size), 0)
    col_ids = lax.broadcasted_iota(jnp.int32, (size, size), 1)
    eye = (row_ids == col_ids).astype(F32)
    width = min(SEED_BLOCK, size)
    power = jnp.where(row_ids // width == col_ids // width, -strict, 0.0)
    inverse = eye + power
    reach = 2
    while reach < width:
        power = exact_dot(power, power)
        inverse = inverse + exact_dot(inverse, power)
        reach *= 2
    while width < size:
        inside = row_ids // (2 * width) == col_ids // (2 * width)
        across = row_ids // width != col_ids // width
        corner = jnp.where(inside & across, strict, 0.0)
        inverse = inverse - exact_dot(exact_dot(inverse, corner), inverse)
        width *= 2
    return inverse


def kernel(
    rows, cols,
    rhs_hbm, diag_hbm, off_hbm, target, source, position, count,
    out_ref,
    rhs, diag, off, inverse_parts, scale, off_parts, landed, known, partial, arrived,
    load_sem, col_send, col_recv, row_send, row_recv,
):
    levels, nrhs, size = rhs.shape
    slots = off.shape[1]
    my_row, my_col = lax.axis_index("row"), lax.axis_index("col")
    part_rows = nrhs // CHAINS

    loads = [
        pltpu.make_async_copy(diag_hbm.at[0, 0, 0], diag.at[0], load_sem.at[0]),
        pltpu.make_async_copy(rhs_hbm.at[:, 0, 0], rhs, load_sem.at[1]),
        pltpu.make_async_copy(diag_hbm.at[1:, 0, 0], diag.at[1:], load_sem.at[2]),
    ]
    off_loads = [
        pltpu.make_async_copy(off_hbm.at[0, 0, step], off.at[step], load_sem.at[3 + step])
        for step in range(levels - 1)
    ]
    for load in loads + off_loads:
        load.start()

    barrier = pltpu.get_barrier_semaphore()
    for shift in range(1, cols):
        pl.semaphore_signal(
            barrier, inc=1, device_id={"col": lax.rem(my_col + shift, cols)},
            device_id_type=pl.DeviceIdType.MESH,
        )
    for shift in range(1, rows):
        pl.semaphore_signal(
            barrier, inc=1, device_id={"row": lax.rem(my_row + shift, rows)},
            device_id_type=pl.DeviceIdType.MESH,
        )

    def col_copy(step, part, shift):
        return pltpu.make_async_remote_copy(
            src_ref=landed.at[step, part, 0],
            dst_ref=landed.at[step, part, shift],
            send_sem=col_send.at[step, part, shift],
            recv_sem=col_recv.at[step, part, shift],
            device_id={"col": lax.rem(my_col + shift, cols)},
            device_id_type=pl.DeviceIdType.MESH,
        )

    def row_copy(step, part, shift):
        return pltpu.make_async_remote_copy(
            src_ref=partial.at[step, part, shift],
            dst_ref=arrived.at[step, part, shift],
            send_sem=row_send.at[step, part, shift],
            recv_sem=row_recv.at[step, part, shift],
            device_id={"row": lax.rem(my_row + shift, rows)},
            device_id_type=pl.DeviceIdType.MESH,
        )

    def invert(step):
        upper = diag[step].T
        row_ids = lax.broadcasted_iota(jnp.int32, (size, size), 0)
        col_ids = lax.broadcasted_iota(jnp.int32, (size, size), 1)
        inverse_main = 1.0 / jnp.sum(
            jnp.where(row_ids == col_ids, upper, 0.0), axis=0, keepdims=True
        )
        strict = jnp.where(row_ids < col_ids, upper, 0.0) * inverse_main
        high, low = split_parts(unit_upper_inverse(strict))
        inverse_parts[step, :, :size] = high
        inverse_parts[step, :, size:] = low
        scale[step] = jnp.broadcast_to(inverse_main, scale.shape[1:])

    def split_off(step):
        off_loads[step].wait()
        for slot in range(slots):
            high, low = split_parts(off[step, slot])
            off_parts[slot, :size, :] = high
            off_parts[slot, size:, :] = low

    def four_terms(full):
        return (full[:part_rows, :size] + full[part_rows:, size:]) + (
            full[:part_rows, size:] + full[part_rows:, :size]
        )

    def solve(step, part):
        span = pl.ds(part * part_rows, part_rows)
        reduced = rhs[step, span]
        if step > 0:
            coupling = partial[step - 1, part, 0]
            for shift in range(1, rows):
                row_copy(step - 1, part, shift).wait_recv()
                coupling = coupling + arrived[step - 1, part, shift]
            reduced = reduced - coupling
        high, low = split_parts(reduced * scale[step, :1])
        full = jnp.dot(
            jnp.concatenate([high, low], axis=0), inverse_parts[step],
            preferred_element_type=F32,
        )
        current = four_terms(full)
        if step + 1 < levels:
            landed[step, part, 0] = current
        out_ref[step, 0, 0, span] = current

    def send_cols(step, part):
        for shift in range(cols - 1, 0, -1):
            col_copy(step, part, shift).start()

    def collect(step, part):
        for shift in range(cols):
            if shift > 0:
                col_copy(step, part, shift).wait_recv()
            high, low = split_parts(landed[step, part, shift])
            column = lax.rem(my_col + cols - shift, cols)
            known[part, step, column, :part_rows] = high
            known[part, step, column, part_rows:] = low

    def products(step, part):
        held = []
        for slot in range(slots):
            operand = known[part, source[0, 0, step, slot], position[0, 0, step, slot]]
            full = lax.dot_general(
                operand, off_parts[slot], (((1,), (1,)), ((), ())), preferred_element_type=F32
            )
            held.append(four_terms(full))
        used = count[0, 0, step]
        for shift in range(rows):
            row = lax.rem(my_row + shift, rows)
            total = None
            for slot in range(slots):
                here = (target[0, 0, step, slot] == row) & (slot < used)
                term = held[slot] * jnp.where(here, 1.0, 0.0).astype(F32)
                total = term if total is None else total + term
            partial[step, part, shift] = total

    def send_rows(step, part):
        for shift in range(1, rows):
            row_copy(step, part, shift).start()

    loads[0].wait()
    invert(0)
    loads[1].wait()
    pl.semaphore_wait(barrier, rows + cols - 2)
    for step in range(levels):
        for part in range(CHAINS):
            solve(step, part)
            if step + 1 < levels:
                send_cols(step, part)
        if step + 1 < levels:
            split_off(step)
            for part in range(CHAINS):
                collect(step, part)
                products(step, part)
                send_rows(step, part)
            if step == 0:
                loads[2].wait()
            invert(step + 1)
    for step in range(levels - 1):
        for part in range(CHAINS):
            for shift in range(1, cols):
                col_copy(step, part, shift).wait_send()
            for shift in range(1, rows):
                row_copy(step, part, shift).wait_send()


def solution(mesh):
    rows, cols = mesh.shape["row"], mesh.shape["col"]

    def per_device(
        right_side, diag_blocks, off_blocks, slot_target, slot_level, slot_position, slot_count
    ):
        levels, nrhs, size = right_side.shape[0], right_side.shape[3], right_side.shape[4]
        slots = off_blocks.shape[3]
        steps, part_rows = levels - 1, nrhs // CHAINS
        anywhere = pl.BlockSpec(memory_space=pl.ANY)
        scalars = pl.BlockSpec(memory_space=pltpu.SMEM)
        return pl.pallas_call(
            functools.partial(kernel, rows, cols),
            out_shape=jax.ShapeDtypeStruct(right_side.shape, F32),
            in_specs=[anywhere] * 3 + [scalars] * 4,
            out_specs=pl.BlockSpec(memory_space=pltpu.VMEM),
            scratch_shapes=[
                pltpu.VMEM((levels, nrhs, size), F32),
                pltpu.VMEM((levels, size, size), F32),
                pltpu.VMEM((steps, slots, size, size), F32),
                pltpu.VMEM((levels, size, 2 * size), BF16),
                pltpu.VMEM((levels, 8, size), F32),
                pltpu.VMEM((slots, 2 * size, size), BF16),
                pltpu.VMEM((steps, CHAINS, cols, part_rows, size), F32),
                pltpu.VMEM((CHAINS, steps, cols, 2 * part_rows, size), BF16),
                pltpu.VMEM((steps, CHAINS, rows, part_rows, size), F32),
                pltpu.VMEM((steps, CHAINS, rows, part_rows, size), F32),
                pltpu.SemaphoreType.DMA((3 + steps,)),
                pltpu.SemaphoreType.DMA((steps, CHAINS, cols)),
                pltpu.SemaphoreType.DMA((steps, CHAINS, cols)),
                pltpu.SemaphoreType.DMA((steps, CHAINS, rows)),
                pltpu.SemaphoreType.DMA((steps, CHAINS, rows)),
            ],
            compiler_params=pltpu.CompilerParams(collective_id=0, has_side_effects=True),
            name="level_solve",
        )(
            right_side, diag_blocks, off_blocks,
            slot_target, slot_level, slot_position, slot_count,
        )

    return jax.shard_map(
        per_device,
        mesh=mesh,
        in_specs=(
            P(None, "row", "col", None, None),
            P(None, "row", "col", None, None),
            P("row", "col", None, None, None, None),
            P("row", "col", None, None),
            P("row", "col", None, None),
            P("row", "col", None, None),
            P("row", "col", None),
        ),
        out_specs=P(None, "row", "col", None, None),
        check_vma=False,
    )
```

time: 141 us -> 40.9 us (0.29)
  blocking collectives: 54.3 us -> 0 us
  other arithmetic: 53.4 us -> 0 us
  Pallas kernels: 0 us -> 39.2 us
  starting transfers between devices: 16.3 us -> 0 us
  matrix products: 7.75 us -> 0 us
  local copies, waits for them, and re-layouts: 8.02 us -> 1.53 us
    all_gather x4 -> x0, blocking collectives: 54.3 us -> none  [per_device(): shared = lax.all_gather(current[None], 'col', axis=0, tiled=True)]
    another operation x6 -> x0, other arithmetic: 50 us -> none  [solve_block(): jax.scipy.linalg.solve_triangular(diagonal, right_rows.T, lower=True)]
    pallas_call x0 -> x1, Pallas kernels: none -> 39.2 us  [per_device(): pl.pallas_call(functools.partial(kernel, rows, cols), out_shape=jax.Shape...]
    all_to_all x4 -> x0, starting transfers between devices: 16.3 us -> none  [per_device(): lax.all_to_all(by_target, 'row', split_axis=0, concat_axis=0, tiled=True)]
    dot_general x8 -> x0, matrix products: 6.23 us -> none  [the longest x4 4.89 us: slot_products(): jnp.einsum('snb,sab->sna', operands, blocks, precision=lax.Precision.HIGH...]
    dot_general x4 -> x0, local copies, waits for them, and re-layouts: 2.71 us -> none  [per_device(): jnp.einsum('st,sna->tna', selector, pending, precision=lax.Precision.HIGH...]
    convert_element_type x4 -> x0, other arithmetic: 2.47 us -> none  [per_device(): active.astype(jnp.float32)]
    gather x4 -> x0, local copies, waits for them, and re-layouts: 2.29 us -> none  [slot_products(): operands = gathered[source_ids, source_cols] * weights[:, None, None]]
  transfers between devices with their start and end apart: 4 -> 0, of which waited for: 0 -> 0; matrix products, arithmetic and copies ran while one was open for 29% -> 0% of each run, Pallas kernels for 0% -> 0%
where the time goes in v1:
time: 40.9 us; the launch traced here: 40.7 us
  Pallas kernels  39.2 us (96%)
  local copies, waits for them, and re-layouts  1.53 us (4%)
    pallas_call x1, Pallas kernels, per_device(): pl.pallas_call(functools.partial(kernel, rows, cols), out_shape=jax.Shape...  39.2 us
    unnamed x1, local copies, waits for them, and re-layouts  1.53 us

profile of v1, /device:TPU:0, one launch (start us, length us, event | category | flops | bytes accessed | tf_op | source)
XLA Modules:
  0.0 40.7 jit_solution(17207087003043817366)
XLA Ops:
  0.0 39.2 %level_solve.1 = f32[5,1,1,32,128]{4,3,2,1,0:T(8,128)} custom-call(f32[5,1,1,32,128]{4,3,2,1,0:T(8,128)} %rhs_hbm.1, f32[5,1,1,128,128]{4,3,2,1,0:T(8,128)} %diag_hbm.1, f32[1,1,4,8,128,128]{5,4,3,2,1,0:T(8,128)} %off_hbm.1, s32[1,1,4,8]{3,2,1,0:T(4,128)} %target.1, s32[1,1,4,8]{3,2,1,0:T(4,128)} %source.1, s32[1,1,4,8]{3,2,1,0:T(4,128)} %position.1, ...), custom_call_target="tpu_custom_call" | custom-call | tf_op jit(solution)/shard_map/level_solve/pallas_call | solution.py:219
  39.2 1.5 %copy.9 = f32[5,1,1,32,128]{4,3,2,1,0:T(8,128)} copy(f32[5,1,1,32,128]{4,3,2,1,0:T(8,128)} %level_solve.1) | data formatting | bytes 163840

commit v2 on v1

--- a/solution.py
+++ b/solution.py
@@ -10,7 +10,7 @@
 F32 = jnp.float32
 BF16 = jnp.bfloat16
 SEED_BLOCK = 32
-CHAINS = 1
+CHAINS = 2
 
 
 def split_parts(value):
@@ -46,10 +46,11 @@
 
 def kernel(
     rows, cols,
-    rhs_hbm, diag_hbm, off_hbm, target, source, position, count,
+    rhs_hbm, diag_hbm, off_hbm, target_hbm, source_hbm, position_hbm, count_hbm,
     out_ref,
     rhs, diag, off, inverse_parts, scale, off_parts, landed, known, partial, arrived,
-    load_sem, col_send, col_recv, row_send, row_recv,
+    target, source, position, count, weights,
+    load_sem, index_sem, col_send, col_recv, row_send, row_recv,
 ):
     levels, nrhs, size = rhs.shape
     slots = off.shape[1]
@@ -65,7 +66,13 @@
         pltpu.make_async_copy(off_hbm.at[0, 0, step], off.at[step], load_sem.at[3 + step])
         for step in range(levels - 1)
     ]
-    for load in loads + off_loads:
+    index_loads = [
+        pltpu.make_async_copy(source_ref, held_ref, index_sem.at[i])
+        for i, (source_ref, held_ref) in enumerate(
+            [(target_hbm, target), (source_hbm, source), (position_hbm, position), (count_hbm, count)]
+        )
+    ]
+    for load in loads + index_loads + off_loads:
         load.start()
 
     barrier = pltpu.get_barrier_semaphore()
@@ -157,6 +164,16 @@
             known[part, step, column, :part_rows] = high
             known[part, step, column, part_rows:] = low
 
+    def weigh(step):
+        used = count[0, 0, step]
+        for shift in range(rows):
+            row = lax.rem(my_row + shift, rows)
+            for slot in range(slots):
+                here = (target[0, 0, step, slot] == row) & (slot < used)
+                weights[shift, slot : slot + 1, :] = jnp.full(
+                    (1, size), jnp.where(here, 1.0, 0.0), F32
+                )
+
     def products(step, part):
         held = []
         for slot in range(slots):
@@ -165,19 +182,14 @@
                 operand, off_parts[slot], (((1,), (1,)), ((), ())), preferred_element_type=F32
             )
             held.append(four_terms(full))
-        used = count[0, 0, step]
-        for shift in range(rows):
-            row = lax.rem(my_row + shift, rows)
+        for shift in range(rows - 1, -1, -1):
             total = None
             for slot in range(slots):
-                here = (target[0, 0, step, slot] == row) & (slot < used)
-                term = held[slot] * jnp.where(here, 1.0, 0.0).astype(F32)
+                term = held[slot] * weights[shift, slot : slot + 1, :]
                 total = term if total is None else total + term
             partial[step, part, shift] = total
-
-    def send_rows(step, part):
-        for shift in range(1, rows):
-            row_copy(step, part, shift).start()
+            if shift > 0:
+                row_copy(step, part, shift).start()
 
     loads[0].wait()
     invert(0)
@@ -189,11 +201,14 @@
             if step + 1 < levels:
                 send_cols(step, part)
         if step + 1 < levels:
+            if step == 0:
+                for load in index_loads:
+                    load.wait()
             split_off(step)
+            weigh(step)
             for part in range(CHAINS):
                 collect(step, part)
                 products(step, part)
-                send_rows(step, part)
             if step == 0:
                 loads[2].wait()
             invert(step + 1)
@@ -215,11 +230,10 @@
         slots = off_blocks.shape[3]
         steps, part_rows = levels - 1, nrhs // CHAINS
         anywhere = pl.BlockSpec(memory_space=pl.ANY)
-        scalars = pl.BlockSpec(memory_space=pltpu.SMEM)
         return pl.pallas_call(
             functools.partial(kernel, rows, cols),
             out_shape=jax.ShapeDtypeStruct(right_side.shape, F32),
-            in_specs=[anywhere] * 3 + [scalars] * 4,
+            in_specs=[anywhere] * 7,
             out_specs=pl.BlockSpec(memory_space=pltpu.VMEM),
             scratch_shapes=[
                 pltpu.VMEM((levels, nrhs, size), F32),
@@ -232,7 +246,13 @@
                 pltpu.VMEM((CHAINS, steps, cols, 2 * part_rows, size), BF16),
                 pltpu.VMEM((steps, CHAINS, rows, part_rows, size), F32),
                 pltpu.VMEM((steps, CHAINS, rows, part_rows, size), F32),
+                pltpu.SMEM(slot_target.shape, jnp.int32),
+                pltpu.SMEM(slot_level.shape, jnp.int32),
+                pltpu.SMEM(slot_position.shape, jnp.int32),
+                pltpu.SMEM(slot_count.shape, jnp.int32),
+                pltpu.VMEM((rows, slots, size), F32),
                 pltpu.SemaphoreType.DMA((3 + steps,)),
+                pltpu.SemaphoreType.DMA((4,)),
                 pltpu.SemaphoreType.DMA((steps, CHAINS, cols)),
                 pltpu.SemaphoreType.DMA((steps, CHAINS, cols)),
                 pltpu.SemaphoreType.DMA((steps, CHAINS, rows)),

time: 40.9 us -> 39.8 us (0.973)
  Pallas kernels: 39.2 us -> 38.1 us
    pallas_call x1, Pallas kernels: 39.2 us -> 38.1 us  [per_device(): pl.pallas_call(functools.partial(kernel, rows, cols), out_shape=jax.Shape...]
where the time goes in v2:
time: 39.8 us; the launch traced here: 39.6 us
  Pallas kernels  38.1 us (96%)
  local copies, waits for them, and re-layouts  1.53 us (4%)
    pallas_call x1, Pallas kernels, per_device(): pl.pallas_call(functools.partial(kernel, rows, cols), out_shape=jax.Shape...  38.1 us
    unnamed x1, local copies, waits for them, and re-layouts  1.53 us

profile of v2, /device:TPU:0, one launch (start us, length us, event | category | flops | bytes accessed | tf_op | source)
XLA Modules:
  0.0 39.6 jit_solution(16389476342611309074)
XLA Ops:
  0.0 38.1 %level_solve.1 = f32[5,1,1,32,128]{4,3,2,1,0:T(8,128)} custom-call(f32[5,1,1,32,128]{4,3,2,1,0:T(8,128)} %rhs_hbm.1, f32[5,1,1,128,128]{4,3,2,1,0:T(8,128)} %diag_hbm.1, f32[1,1,4,8,128,128]{5,4,3,2,1,0:T(8,128)} %off_hbm.1, s32[1,1,4,8]{3,2,1,0:T(4,128)} %target_hbm.1, s32[1,1,4,8]{3,2,1,0:T(4,128)} %source_hbm.1, s32[1,1,4,8]{3,2,1,0:T(4,128)} %position_hbm.1, ...), custom_call_target="tpu_custom_call" | custom-call | tf_op jit(solution)/shard_map/level_solve/pallas_call | solution.py:233
  38.1 1.5 %copy.9 = f32[5,1,1,32,128]{4,3,2,1,0:T(8,128)} copy(f32[5,1,1,32,128]{4,3,2,1,0:T(8,128)} %level_solve.1) | data formatting | bytes 163840
